TPU v7x, 256 devices: a whole 4x4x8 slice. The times are simulated.
256 devices in a mesh: blk: 128 (over z, y, x_lo, core), head: 2 (over x_hi).
Axes of the slice: x: 4 (x_hi: 2, x_lo: 2; x = x_hi * 2 + x_lo), y: 4, z: 8, core: 2. Of those that a mesh axis runs over, the one named last changes fastest.
Arguments:
- queries: bfloat16 [65536, 16, 128], P('blk', 'head'), may hold values from -6 to 6
- out_grad: bfloat16 [65536, 16, 128], P('blk', 'head'), may hold values from -6 to 6
- outputs: bfloat16 [65536, 16, 128], P('blk', 'head'), may hold values from -6 to 6
- key_vectors: bfloat16 [65536, 128], P('blk'), may hold values from -6 to 6
- value_vectors: bfloat16 [65536, 128], P('blk'), may hold values from -6 to 6
- logsumexp: float32 [65536, 16], P('blk', 'head'), may hold values from 4 to 7
- positions: int32 [65536], P('blk'), may hold values from 0 to 65535, as said below
- doc_start: int32 [65536], P('blk'), may hold values from 0 to 65535, as said below
Outputs:
- query_grad: bfloat16 [65536, 16, 128], P('blk', 'head')
- key_grad: bfloat16 [65536, 128], P('blk')
- value_grad: bfloat16 [65536, 128], P('blk')
Inputs may be any that keep to these rules, and one draw needn't show every extreme that they name: positions is a permutation of 0 to 65535; row r holds position (r mod 512) * 128 + sigma(r div 512), sigma a permutation of the blocks of 512 rows. doc_start of a row is the first position of the document that holds the row's position; documents are runs of consecutive positions, the first starting at 0, and the last position starts a document of its own.
All inputs are finite; a program needn't handle non-finite values.
Results may differ from a plain program's by a relative error of at most 0.0063.
Values may be sent and summed in bfloat16 or wider, within the bound.
A program may use at most 64 MiB of HBM per device.

v0:
```python
import functools
import math

import jax
import jax.numpy as jnp
from jax import lax
from jax.experimental import pallas as pl
from jax.experimental.pallas import tpu as pltpu
from jax.sharding import PartitionSpec as P

MESH = pl.DeviceIdType.MESH
STEPS = 4
TOK = 512
HEADS = 8
HD = 128
ROWS = TOK * HEADS
CHUNK = 512
N_CHUNK = ROWS // CHUNK
TILE = 128
EXP2 = math.log2(math.e)
SCALE = HD**-0.5


def tiles_of(chunk):
    last = (chunk + 1) * CHUNK // HEADS
    return -(-last // TILE)


def scores_of(chunk, qdo, weights, sdp):
    width = 2 * TILE * tiles_of(chunk)
    sdp[:, :width] = jnp.dot(
        qdo[chunk * CHUNK : (chunk + 1) * CHUNK, :],
        weights[:, :width],
        preferred_element_type=jnp.float32,
    )


def attend_of(chunk, sdp, lse_b, delta_b, start_b, width_b, key_pos, p_out, d_out):
    piece = 64
    for at in range(0, CHUNK, piece):
        here = slice(at, at + piece)
        rows = slice(chunk * CHUNK + at, chunk * CHUNK + at + piece)
        lse, delta = lse_b[rows, :], delta_b[rows, :]
        start, width = start_b[rows, :], width_b[rows, :]
        for j in range(tiles_of(chunk)):
            keys = slice(j * TILE, (j + 1) * TILE)
            s = sdp[here, 2 * j * TILE : (2 * j + 1) * TILE]
            dp = sdp[here, (2 * j + 1) * TILE : (2 * j + 2) * TILE]
            after = (key_pos[j : j + 1, :] - start).astype(jnp.uint32)
            p = jnp.where(after <= width, jnp.exp2(s * (SCALE * EXP2) - lse), 0.0)
            p_out[here, keys] = p.astype(jnp.bfloat16)
            d_out[here, keys] = (p * (dp - delta)).astype(jnp.bfloat16)


def grads_of(chunk, p_in, d_in, qdo_t, keys, acc, dq):
    nk = tiles_of(chunk) * TILE
    rows = slice(chunk * CHUNK, (chunk + 1) * CHUNK)
    acc[HD:, :nk] += jnp.dot(qdo_t[HD:, rows], p_in[:, :nk], preferred_element_type=jnp.float32)
    acc[:HD, :nk] += jnp.dot(qdo_t[:HD, rows], d_in[:, :nk], preferred_element_type=jnp.float32)
    dq[rows, :] += jnp.dot(d_in[:, :nk], keys[:nk, :], preferred_element_type=jnp.float32)


def kernel(
    comm,
    n_blk,
    pos_smem,
    start_smem,
    q_hbm,
    do_hbm,
    o_hbm,
    k_hbm,
    v_hbm,
    lse_hbm,
    pos_hbm,
    dq_out,
    dk_out,
    dv_out,
    qdo,
    o_buf,
    lse_in,
    kv,
    pos,
    qdo_t,
    lse_b,
    delta_b,
    start_b,
    width_b,
    weights,
    sdp_a,
    sdp_b,
    p_a,
    p_b,
    d_a,
    d_b,
    acc,
    dq,
    dq_low,
    grad_low,
    part,
    inbox,
    load_sem,
    kv_send,
    kv_recv,
    pos_send,
    pos_recv,
    part_send,
    part_recv,
    out_sem,
):
    if comm:
        blk, head = lax.axis_index("blk"), lax.axis_index("head")
    else:
        blk, head = 0, 0
    odd = lax.rem(blk, 2) == 1 if comm else None

    def device(shift):
        return (lax.rem(blk + shift + n_blk, n_blk), head)

    loads = [
        pltpu.make_async_copy(k_hbm, kv.at[0, 0:TOK, :], load_sem.at[0]),
        pltpu.make_async_copy(v_hbm, kv.at[0, TOK : 2 * TOK, :], load_sem.at[1]),
        pltpu.make_async_copy(pos_hbm, pos.at[0], load_sem.at[2]),
        pltpu.make_async_copy(do_hbm, qdo.at[:, HD : 2 * HD], load_sem.at[3]),
        pltpu.make_async_copy(o_hbm, o_buf, load_sem.at[4]),
        pltpu.make_async_copy(q_hbm, qdo.at[:, 0:HD], load_sem.at[5]),
        pltpu.make_async_copy(lse_hbm, lse_in, load_sem.at[6]),
    ]
    for load in loads:
        load.start()

    def kv_copy(src, dst, send, shift):
        to = device(shift)
        return (
            pltpu.make_async_remote_copy(
                kv.at[src], kv.at[dst], kv_send.at[send], kv_recv.at[dst], to, MESH
            ),
            pltpu.make_async_remote_copy(
                pos.at[src], pos.at[dst], pos_send.at[send], pos_recv.at[dst], to, MESH
            ),
        )

    def start_kv(*args):
        for copy in kv_copy(*args):
            copy.start()

    def wait_kv_send(*args):
        for copy in kv_copy(*args):
            copy.wait_send()

    def part_copy(src, dst, shift):
        return pltpu.make_async_remote_copy(
            part.at[src], inbox.at[dst], part_send.at[src], part_recv.at[dst], device(shift), MESH
        )

    twin = (blk, 1 - head)

    if comm:
        barrier = pltpu.get_barrier_semaphore()
        for shift in (-3, -2, -1, 1, 2, 3):
            pl.semaphore_signal(barrier, inc=1, device_id=device(shift), device_id_type=MESH)
        pl.semaphore_signal(barrier, inc=1, device_id=twin, device_id_type=MESH)
        pl.semaphore_wait(barrier, 7)
    for load in loads[:3]:
        load.wait()
    if comm:
        start_kv(0, 1, 0, -1)

    def spread(t, carry):
        first = start_smem[t]
        at = pl.multiple_of(t * HEADS, HEADS)
        start_b[pl.ds(at, HEADS), :] = jnp.full((HEADS, TILE), first, jnp.int32)
        width_b[pl.ds(at, HEADS), :] = jnp.full(
            (HEADS, TILE), pos_smem[t] - first, jnp.int32
        ).astype(jnp.uint32)
        return carry

    lax.fori_loop(0, TOK, spread, 0, unroll=8)

    weights[...] = jnp.zeros_like(weights)

    loads[6].wait()
    lse_t = jnp.swapaxes(lse_in[...], 0, 1) * EXP2
    for t in range(TOK):
        lse_b[t * HEADS : (t + 1) * HEADS, :] = jnp.broadcast_to(
            lse_t[:, t : t + 1], (HEADS, TILE)
        )

    for load in loads[3:6]:
        load.wait()

    def prepare(i, carry):
        rows = pl.ds(pl.multiple_of(i * 256, 256), 256)
        grad = qdo[rows, HD:]
        delta = jnp.sum(
            grad.astype(jnp.float32) * o_buf[rows, :].astype(jnp.float32), axis=1, keepdims=True
        )
        delta_b[rows, :] = jnp.broadcast_to(delta, (256, TILE))
        qdo_t[HD:, rows] = jnp.swapaxes(grad, 0, 1)
        qdo_t[:HD, rows] = jnp.swapaxes(qdo[rows, :HD], 0, 1)
        return carry

    lax.fori_loop(0, ROWS // 256, prepare, 0)
    dq[...] = jnp.zeros_like(dq)

    def step(turn, carry):
        slot = lax.rem(turn + 1, STEPS)
        if comm:

            @pl.when(turn < STEPS - 1)
            def _():
                for copy in kv_copy(slot, slot, 0, 0):
                    copy.wait_recv()

            @pl.when(jnp.logical_and(turn == 0, odd))
            def _():
                start_kv(0, 2, 1, -2)
                start_kv(1, 2, 2, -1)

            @pl.when(jnp.logical_and(turn == 1, odd))
            def _():
                start_kv(2, 3, 3, -1)

            @pl.when(jnp.logical_and(turn == 1, jnp.logical_not(odd)))
            def _():
                start_kv(0, 3, 1, -3)

        keys = kv.at[slot, 0:TOK, :]
        values = kv.at[slot, TOK : 2 * TOK, :]
        key_pos = pos[slot]
        for j in range(TOK // TILE):
            rows = slice(j * TILE, (j + 1) * TILE)
            at = 2 * j * TILE
            weights[:HD, at : at + TILE] = jnp.swapaxes(keys[rows, :], 0, 1)
            weights[HD:, at + TILE : at + 2 * TILE] = jnp.swapaxes(values[rows, :], 0, 1)
        acc[...] = jnp.zeros_like(acc)
        sdp, p_bf, d_bf = (sdp_a, sdp_b), (p_a, p_b), (d_a, d_b)
        for c in range(-1, N_CHUNK + 1):
            if c + 1 < N_CHUNK:
                scores_of(c + 1, qdo, weights, sdp[(c + 1) % 2])
            if 0 <= c < N_CHUNK:
                attend_of(
                    c, sdp[c % 2], lse_b, delta_b, start_b, width_b, key_pos, p_bf[c % 2], d_bf[c % 2]
                )
            if c >= 1:
                grads_of(c - 1, p_bf[(c - 1) % 2], d_bf[(c - 1) % 2], qdo_t, keys, acc, dq)

        if comm:

            @pl.when(turn == 0)
            def _():
                part[0] = acc[...].astype(jnp.bfloat16)

                @pl.when(odd)
                def _():
                    part_copy(0, 0, -1).start()

                @pl.when(jnp.logical_not(odd))
                def _():
                    part_copy(0, 2, 1).start()

            @pl.when(turn == 1)
            def _():
                @pl.when(odd)
                def _():
                    part[1] = acc[...].astype(jnp.bfloat16)
                    part_copy(1, 1, -1).start()

                @pl.when(jnp.logical_not(odd))
                def _():
                    part_copy(0, 0, 0).wait_recv()
                    part[1] = (acc[...] + inbox[0].astype(jnp.float32)).astype(jnp.bfloat16)
                    part_copy(1, 2, 2).start()

            @pl.when(turn == 2)
            def _():
                @pl.when(odd)
                def _():
                    part[2] = acc[...].astype(jnp.bfloat16)

                @pl.when(jnp.logical_not(odd))
                def _():
                    part_copy(0, 1, 0).wait_recv()
                    part[2] = (acc[...] + inbox[1].astype(jnp.float32)).astype(jnp.bfloat16)

                part_copy(2, 3, 3).start()

        return carry

    lax.fori_loop(0, STEPS, step, 0)

    twin_copy = pltpu.make_async_remote_copy(
        part.at[3], inbox.at[4], part_send.at[3], part_recv.at[4], twin, MESH
    )
    if comm:
        part_copy(0, 2, 0).wait_recv()
        part_copy(0, 3, 0).wait_recv()
        part[3] = (
            acc[...] + inbox[2].astype(jnp.float32) + inbox[3].astype(jnp.float32)
        ).astype(jnp.bfloat16)
        twin_copy.start()
    else:
        part[3] = acc[...].astype(jnp.bfloat16)
    for i in range(N_CHUNK):
        rows = slice(i * CHUNK, (i + 1) * CHUNK)
        dq_low[rows, :] = (dq[rows, :] * SCALE).astype(jnp.bfloat16)
    outs = [pltpu.make_async_copy(dq_low, dq_out, out_sem.at[0])]
    outs[0].start()
    if comm:
        twin_copy.wait_recv()
        total = part[3].astype(jnp.float32) + inbox[4].astype(jnp.float32)
    else:
        total = part[3].astype(jnp.float32)
    grad_low[0] = jnp.swapaxes(total[:HD] * SCALE, 0, 1).astype(jnp.bfloat16)
    grad_low[1] = jnp.swapaxes(total[HD:], 0, 1).astype(jnp.bfloat16)
    outs.append(pltpu.make_async_copy(grad_low.at[0], dk_out, out_sem.at[1]))
    outs.append(pltpu.make_async_copy(grad_low.at[1], dv_out, out_sem.at[2]))
    outs[1].start()
    outs[2].start()
    if comm:
        wait_kv_send(0, 1, 0, -1)

        @pl.when(odd)
        def _():
            wait_kv_send(0, 2, 1, -2)
            wait_kv_send(1, 2, 2, -1)
            wait_kv_send(2, 3, 3, -1)
            part_copy(0, 0, -1).wait_send()
            part_copy(1, 1, -1).wait_send()

        @pl.when(jnp.logical_not(odd))
        def _():
            wait_kv_send(0, 3, 1, -3)
            part_copy(0, 2, 1).wait_send()
            part_copy(1, 2, 2).wait_send()

        part_copy(2, 3, 3).wait_send()
        twin_copy.wait_send()
    for out in outs:
        out.wait()


def call(comm, n_blk, q, do, o, k, v, lse, pos, start):
    any_space = pl.BlockSpec(memory_space=pl.ANY)
    smem = pl.BlockSpec(memory_space=pltpu.SMEM)
    flat = (ROWS, HD)
    low, full = jnp.bfloat16, jnp.float32
    dq, dk, dv = pl.pallas_call(
        functools.partial(kernel, comm, n_blk),
        out_shape=(
            jax.ShapeDtypeStruct(flat, low),
            jax.ShapeDtypeStruct(k.shape, low),
            jax.ShapeDtypeStruct(v.shape, low),
        ),
        in_specs=[smem, smem] + [any_space] * 7,
        out_specs=(any_space,) * 3,
        scratch_shapes=[
            pltpu.VMEM((ROWS, 2 * HD), low),
            pltpu.VMEM(flat, low),
            pltpu.VMEM((TOK, HEADS), full),
            pltpu.VMEM((STEPS, 2 * TOK, HD), low),
            pltpu.VMEM((STEPS, TOK // TILE, TILE), jnp.int32),
            pltpu.VMEM((2 * HD, ROWS), low),
            pltpu.VMEM(flat, full),
            pltpu.VMEM(flat, full),
            pltpu.VMEM(flat, jnp.int32),
            pltpu.VMEM(flat, jnp.uint32),
            pltpu.VMEM((2 * HD, 2 * TOK), low),
            pltpu.VMEM((CHUNK, 2 * TOK), full),
            pltpu.VMEM((CHUNK, 2 * TOK), full),
            pltpu.VMEM((CHUNK, TOK), low),
            pltpu.VMEM((CHUNK, TOK), low),
            pltpu.VMEM((CHUNK, TOK), low),
            pltpu.VMEM((CHUNK, TOK), low),
            pltpu.VMEM((2 * HD, TOK), full),
            pltpu.VMEM(flat, full),
            pltpu.VMEM(flat, low),
            pltpu.VMEM((2, TOK, HD), low),
            pltpu.VMEM((4, 2 * HD, TOK), low),
            pltpu.VMEM((5, 2 * HD, TOK), low),
            pltpu.SemaphoreType.DMA((7,)),
            pltpu.SemaphoreType.DMA((4,)),
            pltpu.SemaphoreType.DMA((4,)),
            pltpu.SemaphoreType.DMA((4,)),
            pltpu.SemaphoreType.DMA((4,)),
            pltpu.SemaphoreType.DMA((4,)),
            pltpu.SemaphoreType.DMA((5,)),
            pltpu.SemaphoreType.DMA((3,)),
        ],
        compiler_params=pltpu.CompilerParams(
            collective_id=0 if comm else None,
            has_side_effects=True,
            vmem_limit_bytes=56 * 1024 * 1024,
        ),
    )(
        pos,
        start,
        q.reshape(flat),
        do.reshape(flat),
        o.reshape(flat),
        k,
        v,
        lse,
        pos.reshape(TOK // TILE, TILE),
    )
    return dq.reshape(q.shape), dk, dv


def solution(mesh):
    n_blk = mesh.shape["blk"]
    in_specs = (
        P("blk", "head", None),
        P("blk", "head", None),
        P("blk", "head", None),
        P("blk", None),
        P("blk", None),
        P("blk", "head"),
        P("blk"),
        P("blk"),
    )
    out_specs = (P("blk", "head", None), P("blk", None), P("blk", None))
    return jax.shard_map(
        functools.partial(call, True, n_blk),
        mesh=mesh,
        in_specs=in_specs,
        out_specs=out_specs,
        check_vma=False,
    )
```

profile of v0, /device:TPU:1, one launch (start us, length us, event | category | flops | bytes accessed | tf_op | source)
XLA Modules:
  0.0 55.8 jit_solution(651737291193432910)
XLA Ops:
  0.6 1.6 %copy.11.lse_hbm = f32[512,8]{1,0:T(8,128)} copy(f32[512,8]{0,1:T(8,128)} %param.13) | data formatting | bytes 32768 | tf_op args[5]
  2.2 49.6 %shard_map.103 = (bf16[4096,128]{1,0:T(8,128)(2,1)}, bf16[512,128]{1,0:T(8,128)(2,1)}, bf16[512,128]{1,0:T(8,128)(2,1)}) custom-call(s32[512]{0:T(512)} %pos_smem.1, s32[512]{0:T(512)} %start_smem.1, bf16[4096,128]{1,0:T(8,128)(2,1)} %bitcast.6, bf16[4096,128]{1,0:T(8,128)(2,1)} %bitcast.7, bf16[4096,128]{1,0:T(8,128)(2,1)} %bitcast.8, ...), custom_call_target="tpu_custom_call" | custom-call | tf_op jit(solution)/shard_map/pallas_call | solution.py:347
  51.8 0.0 copy-start.1
  51.9 2.3 %copy.15 = bf16[512,8,128]{2,1,0:T(8,128)(2,1)} copy(bf16[512,8,128]{2,1,0:T(8,128)(2,1)} %bitcast.5) | data formatting | bytes 2097152
  54.1 0.0 copy-done.1
  54.2 0.0 copy-start
  54.2 0.7 %copy.16 = bf16[512,128]{1,0:T(8,128)(2,1)} copy(bf16[512,128]{1,0:T(8,128)(2,1)S(1)} %copy-done.1) | data formatting | bytes 262144
  54.8 0.3 copy-done
  55.1 0.7 %copy.17 = bf16[512,128]{1,0:T(8,128)(2,1)} copy(bf16[512,128]{1,0:T(8,128)(2,1)S(1)} %copy-done) | data formatting | bytes 262144
Async XLA Ops:
  51.8 2.3 %copy-start.1 = (bf16[512,128]{1,0:T(8,128)(2,1)S(1)}, bf16[512,128]{1,0:T(8,128)(2,1)}, u32[]{:S(2)}) copy-start(bf16[512,128]{1,0:T(8,128)(2,1)} %get-tuple-element.13) | copy-start | bytes 393220
  54.2 1.0 %copy-start = (bf16[512,128]{1,0:T(8,128)(2,1)S(1)}, bf16[512,128]{1,0:T(8,128)(2,1)}, u32[]{:S(2)}) copy-start(bf16[512,128]{1,0:T(8,128)(2,1)} %get-tuple-element.14) | copy-start | bytes 393220
where the time goes:
time: 56 us; the launch traced here: 55.8 us
  Pallas kernels  49.6 us (89%)
  local copies, waits for them, and re-layouts  5.46 us (10%)
  between operations  0.65 us (1%)
    pallas_call x1, Pallas kernels, call(): pl.pallas_call(functools.partial(kernel, comm, n_blk), out_shape=(jax.Sha...  49.6 us
    unnamed x8, local copies, waits for them, and re-layouts  5.46 us

commit v1 on v0

v1 whole, which is shorter than its diff:
```python
import functools
import math

import jax
import jax.numpy as jnp
from jax import lax
from jax.experimental import pallas as pl
from jax.experimental.pallas import tpu as pltpu
from jax.sharding import PartitionSpec as P

MESH = pl.DeviceIdType.MESH
STEPS = 4
TOK = 512
HEADS = 8
HD = 128
ROWS = TOK * HEADS
CHUNK = 512
N_CHUNK = ROWS // CHUNK
TILE = 128
EXP2 = math.log2(math.e)
SCALE = HD**-0.5
HALF = 0.5
MATE, BESIDE = 0, 1
NEAR, FAR, TWIN = 0, 2, 4


def tiles_of(chunk):
    last = (chunk + 1) * CHUNK // HEADS
    return -(-last // TILE)


def scores_of(chunk, qdo, weights, sdp):
    width = 2 * TILE * tiles_of(chunk)
    sdp[:, :width] = jnp.dot(
        qdo[chunk * CHUNK : (chunk + 1) * CHUNK, :],
        weights[:, :width],
        preferred_element_type=jnp.float32,
    )


def attend_of(chunk, sdp, lse_b, delta_b, start_b, place_b, key_pos, p_out, d_out):
    piece = 64
    for at in range(0, CHUNK, piece):
        here = slice(at, at + piece)
        rows = slice(chunk * CHUNK + at, chunk * CHUNK + at + piece)
        lse, delta = lse_b[rows, :], delta_b[rows, :]
        start = start_b[rows, :]
        for j in range(tiles_of(chunk)):
            keys = slice(j * TILE, (j + 1) * TILE)
            s = sdp[here, 2 * j * TILE : (2 * j + 1) * TILE]
            dp = sdp[here, (2 * j + 1) * TILE : (2 * j + 2) * TILE]
            at_key = key_pos[j : j + 1, :]
            met = at_key >= start
            if (j + 1) * TILE * HEADS > chunk * CHUNK:
                met = jnp.logical_and(met, at_key <= place_b[rows, :])
            p = jnp.where(met, jnp.exp2(s * (SCALE * EXP2) - lse), 0.0)
            p_out[here, keys] = p.astype(jnp.bfloat16)
            d_out[here, keys] = (p * (dp - delta)).astype(jnp.bfloat16)


def grads_of(chunk, p_in, d_in, qdo_t, keys, acc, dq):
    nk = tiles_of(chunk) * TILE
    rows = slice(chunk * CHUNK, (chunk + 1) * CHUNK)
    acc[1, :, :nk] += jnp.dot(qdo_t[HD:, rows], p_in[:, :nk], preferred_element_type=jnp.float32)
    acc[0, :, :nk] += jnp.dot(qdo_t[:HD, rows], d_in[:, :nk], preferred_element_type=jnp.float32)
    dq[rows, :] += jnp.dot(d_in[:, :nk], keys[:nk, :], preferred_element_type=jnp.float32)


def kernel(
    n_blk,
    pos_in,
    start_in,
    q_hbm,
    do_hbm,
    o_hbm,
    k_hbm,
    v_hbm,
    lse_hbm,
    pos_hbm,
    dq_out,
    dk_out,
    dv_out,
    pos_smem,
    start_smem,
    qdo,
    o_buf,
    lse_in,
    kv,
    pos,
    qdo_t,
    lse_b,
    delta_b,
    start_b,
    place_b,
    weights,
    sdp_a,
    sdp_b,
    p_a,
    p_b,
    d_a,
    d_b,
    acc,
    own,
    dq,
    grad_low,
    part,
    inbox,
    mate_box,
    load_sem,
    kv_send,
    kv_recv,
    pos_send,
    pos_recv,
    part_send,
    part_recv,
    mate_recv,
    last_sem,
):
    blk, head = lax.axis_index("blk"), lax.axis_index("head")
    odd = lax.rem(blk, 2) == 1
    even = jnp.logical_not(odd)

    reach = jnp.where(odd, 2, 3)

    def device(shift, across=0):
        return (lax.rem(blk + shift + n_blk, n_blk), lax.rem(head + across, 2))

    barrier = pltpu.get_barrier_semaphore()

    def greet(*where):
        for shift, across in where:
            pl.semaphore_signal(
                barrier, inc=1, device_id=device(shift, across), device_id_type=MESH
            )

    @pl.when(odd)
    def _():
        greet((1, 0), (2, 0), (3, 0), (-1, 0), (-2, 0), (-2, 1), (0, 1))

    @pl.when(even)
    def _():
        greet((1, 0), (-2, 0), (-2, 1), (-3, 0), (-3, 1), (0, 1))

    loads = [
        pltpu.make_async_copy(k_hbm, kv.at[0, 0:TOK, :], load_sem.at[0]),
        pltpu.make_async_copy(v_hbm, kv.at[0, TOK : 2 * TOK, :], load_sem.at[1]),
        pltpu.make_async_copy(pos_hbm, pos.at[0], load_sem.at[2]),
        pltpu.make_async_copy(pos_in, pos_smem, load_sem.at[7]),
        pltpu.make_async_copy(start_in, start_smem, load_sem.at[8]),
        pltpu.make_async_copy(lse_hbm, lse_in, load_sem.at[3]),
        pltpu.make_async_copy(do_hbm, qdo.at[:, HD : 2 * HD], load_sem.at[4]),
        pltpu.make_async_copy(q_hbm, qdo.at[:, 0:HD], load_sem.at[5]),
        pltpu.make_async_copy(o_hbm, o_buf, load_sem.at[6]),
    ]
    for load in loads:
        load.start()

    def kv_copy(src, dst, send, shift):
        to = device(shift)
        return (
            pltpu.make_async_remote_copy(
                kv.at[src], kv.at[dst], kv_send.at[send], kv_recv.at[dst], to, MESH
            ),
            pltpu.make_async_remote_copy(
                pos.at[src], pos.at[dst], pos_send.at[send], pos_recv.at[dst], to, MESH
            ),
        )

    def start_kv(*args):
        for copy in kv_copy(*args):
            copy.start()

    def wait_kv_send(*args):
        for copy in kv_copy(*args):
            copy.wait_send()

    def wait_kv(slot):
        for copy in kv_copy(slot, slot, 0, 0):
            copy.wait_recv()

    def part_copy(src, dst, shift, across=0):
        return pltpu.make_async_remote_copy(
            part.at[src, lax.rem(head + across, 2)],
            inbox.at[dst],
            part_send.at[src, across],
            part_recv.at[dst],
            device(shift, across),
            MESH,
        )

    def mate_copy(src, dst, shift):
        return pltpu.make_async_remote_copy(
            part.at[src],
            mate_box.at[dst],
            part_send.at[src, 0],
            mate_recv.at[dst],
            device(shift),
            MESH,
        )

    def wait_part(dst):
        part_copy(0, dst, 0).wait_recv()

    def wait_mate(dst):
        mate_copy(0, dst, 0).wait_recv()

    def send_halves(src, dst, shift):
        part_copy(src, dst, shift).start()
        part_copy(src, dst + 1, shift, 1).start()

    def low(x):
        return x.astype(jnp.bfloat16)

    def full(x):
        return x.astype(jnp.float32)

    @pl.when(even)
    def _():
        for load in loads[:3]:
            load.wait()
        pl.semaphore_wait(barrier, 6)
        start_kv(0, 1, 0, -1)

    def spread(t, carry):
        at = pl.multiple_of(t * HEADS, HEADS)
        start_b[pl.ds(at, HEADS), :] = jnp.full((HEADS, TILE), start_smem[t], jnp.int32)
        place_b[pl.ds(at, HEADS), :] = jnp.full((HEADS, TILE), pos_smem[t], jnp.int32)
        return carry

    loads[3].wait()
    loads[4].wait()
    lax.fori_loop(0, TOK, spread, 0, unroll=16)
    weights[...] = jnp.zeros_like(weights)
    loads[5].wait()
    lse_t = lse_in[...] * EXP2
    for t in range(TOK):
        lse_b[t * HEADS : (t + 1) * HEADS, :] = jnp.broadcast_to(
            lse_t[:, t : t + 1], (HEADS, TILE)
        )
    @pl.when(odd)
    def _():
        for load in loads[:3]:
            load.wait()
        pl.semaphore_wait(barrier, 7)
        start_kv(0, 1, 0, -1)

    for load in loads[6:]:
        load.wait()

    def prepare(i, carry):
        rows = pl.ds(pl.multiple_of(i * 512, 512), 512)
        grad = qdo[rows, HD:]
        delta = jnp.sum(
            grad.astype(jnp.float32) * o_buf[rows, :].astype(jnp.float32), axis=1, keepdims=True
        )
        delta_b[rows, :] = jnp.broadcast_to(delta, (512, TILE))
        qdo_t[HD:, rows] = jnp.swapaxes(grad, 0, 1)
        qdo_t[:HD, rows] = jnp.swapaxes(qdo[rows, :HD], 0, 1)
        return carry

    lax.fori_loop(0, ROWS // 512, prepare, 0)
    dq[...] = jnp.zeros_like(dq)

    def work(slot):
        keys = kv.at[slot, 0:TOK, :]
        values = kv.at[slot, TOK : 2 * TOK, :]
        key_pos = pos[slot]
        for j in range(TOK // TILE):
            rows = slice(j * TILE, (j + 1) * TILE)
            at = 2 * j * TILE
            weights[:HD, at : at + TILE] = jnp.swapaxes(keys[rows, :], 0, 1)
            weights[HD:, at + TILE : at + 2 * TILE] = jnp.swapaxes(values[rows, :], 0, 1)
        acc[...] = jnp.zeros_like(acc)
        sdp, p_bf, d_bf = (sdp_a, sdp_b), (p_a, p_b), (d_a, d_b)
        for c in range(-1, N_CHUNK + 1):
            if c + 1 < N_CHUNK:
                scores_of(c + 1, qdo, weights, sdp[(c + 1) % 2])
            if 0 <= c < N_CHUNK:
                attend_of(
                    c, sdp[c % 2], lse_b, delta_b, start_b, place_b, key_pos, p_bf[c % 2], d_bf[c % 2]
                )
            if c >= 1:
                grads_of(c - 1, p_bf[(c - 1) % 2], d_bf[(c - 1) % 2], qdo_t, keys, acc, dq)

    def step(turn, carry):
        slot = jnp.where(jnp.logical_and(odd, turn > 1), 5 - turn, turn)

        @pl.when(turn == 1)
        def _():
            wait_kv(1)

        @pl.when(jnp.logical_and(turn == 1, odd))
        def _():
            start_kv(1, 2, 2, -1)

        @pl.when(jnp.logical_and(turn == 2, odd))
        def _():
            wait_kv(2)
            start_kv(2, 3, 3, -1)
            wait_kv(3)

        @pl.when(jnp.logical_and(turn == 2, even))
        def _():
            wait_kv(2)

        @pl.when(jnp.logical_and(turn == 3, even))
        def _():
            wait_kv(3)

        @pl.when(jnp.logical_and(turn == 3, odd))
        def _():
            wait_mate(BESIDE)
            own[...] += full(mate_box[BESIDE])
            part[3] = low(own[...])
            part_copy(3, TWIN, 0, 1).start()

        work(slot)

        @pl.when(turn == 0)
        def _():
            start_kv(0, reach, 1, -reach)
            own[...] = acc[...]

        @pl.when(jnp.logical_and(turn == 0, even))
        def _():
            part[3] = low(own[...])
            part_copy(3, TWIN, 0, 1).start()

        @pl.when(turn == 1)
        def _():
            part[0] = low(acc[...])

        @pl.when(jnp.logical_and(turn == 1, odd))
        def _():
            mate_copy(0, MATE, -1).start()

        @pl.when(jnp.logical_and(turn == 1, even))
        def _():
            mate_copy(0, BESIDE, 1).start()

        @pl.when(jnp.logical_and(turn == 2, odd))
        def _():
            part[1] = low(acc[...])
            send_halves(1, FAR, 3)

        @pl.when(jnp.logical_and(turn == 2, even))
        def _():
            wait_mate(MATE)
            part[1] = low(acc[...] + full(mate_box[MATE]))
            send_halves(1, NEAR, 2)

        @pl.when(jnp.logical_and(turn == 3, odd))
        def _():
            wait_mate(MATE)
            part[2] = low(acc[...] + full(mate_box[MATE]))
            send_halves(2, FAR, 2)

        @pl.when(jnp.logical_and(turn == 3, even))
        def _():
            part[2] = low(acc[...])
            mate_copy(2, MATE, 1).start()

        return carry

    lax.fori_loop(0, STEPS, step, 0)

    for i in range(N_CHUNK):
        rows = slice(i * CHUNK, (i + 1) * CHUNK)
        dq_out[rows, :] = (dq[rows, :] * (SCALE * HALF)).astype(jnp.bfloat16)

    wait_part(TWIN)
    half = own.at[head]
    half[...] += full(inbox[TWIN])

    @pl.when(even)
    def _():
        wait_part(NEAR)
        wait_part(NEAR + 1)
        half[...] += full(inbox[NEAR]) + full(inbox[NEAR + 1])

    wait_part(FAR)
    wait_part(FAR + 1)
    total = half[...] + (full(inbox[FAR]) + full(inbox[FAR + 1]))
    factor = jnp.where(head == 0, SCALE * HALF, HALF)
    grad_low[head] = low(jnp.swapaxes(total * factor, 0, 1))
    last = pltpu.make_async_remote_copy(
        grad_low.at[head], grad_low.at[head], last_sem.at[0], last_sem.at[1], device(0, 1), MESH
    )
    last.start()
    last.wait()
    dk_out[...] = grad_low[0]
    dv_out[...] = grad_low[1]

    def sent(src, dst, shift, across=0):
        part_copy(src, dst, shift, across).wait_send()

    sent(3, TWIN, 0, 1)
    wait_kv_send(0, 1, 0, -1)
    wait_kv_send(0, reach, 1, -reach)

    @pl.when(odd)
    def _():
        wait_kv_send(1, 2, 2, -1)
        wait_kv_send(2, 3, 3, -1)
        mate_copy(0, MATE, -1).wait_send()
        sent(1, FAR, 3)
        sent(1, FAR + 1, 3, 1)
        sent(2, FAR, 2)
        sent(2, FAR + 1, 2, 1)

    @pl.when(even)
    def _():
        mate_copy(0, BESIDE, 1).wait_send()
        sent(1, NEAR, 2)
        sent(1, NEAR + 1, 2, 1)
        mate_copy(2, MATE, 1).wait_send()


def call(n_blk, q, do, o, k, v, lse, pos, start):
    in_hbm = pl.BlockSpec(memory_space=pltpu.HBM)
    flat = (ROWS, HD)
    low, full = jnp.bfloat16, jnp.float32
    dq, dk, dv = pl.pallas_call(
        functools.partial(kernel, n_blk),
        out_shape=(
            pltpu.VMEM(flat, low),
            pltpu.VMEM(k.shape, low),
            pltpu.VMEM(v.shape, low),
        ),
        in_specs=[in_hbm] * 9,
        out_specs=(pl.BlockSpec(memory_space=pltpu.VMEM),) * 3,
        scratch_shapes=[
            pltpu.SMEM((TOK,), jnp.int32),
            pltpu.SMEM((TOK,), jnp.int32),
            pltpu.VMEM((ROWS, 2 * HD), low),
            pltpu.VMEM(flat, low),
            pltpu.VMEM((HEADS, TOK), full),
            pltpu.VMEM((STEPS, 2 * TOK, HD), low),
            pltpu.VMEM((STEPS, TOK // TILE, TILE), jnp.int32),
            pltpu.VMEM((2 * HD, ROWS), low),
            pltpu.VMEM(flat, full),
            pltpu.VMEM(flat, full),
            pltpu.VMEM(flat, jnp.int32),
            pltpu.VMEM(flat, jnp.int32),
            pltpu.VMEM((2 * HD, 2 * TOK), low),
            pltpu.VMEM((CHUNK, 2 * TOK), full),
            pltpu.VMEM((CHUNK, 2 * TOK), full),
            pltpu.VMEM((CHUNK, TOK), low),
            pltpu.VMEM((CHUNK, TOK), low),
            pltpu.VMEM((CHUNK, TOK), low),
            pltpu.VMEM((CHUNK, TOK), low),
            pltpu.VMEM((2, HD, TOK), full),
            pltpu.VMEM((2, HD, TOK), full),
            pltpu.VMEM(flat, full),
            pltpu.VMEM((2, TOK, HD), low),
            pltpu.VMEM((4, 2, HD, TOK), low),
            pltpu.VMEM((5, HD, TOK), low),
            pltpu.VMEM((2, 2, HD, TOK), low),
            pltpu.SemaphoreType.DMA((9,)),
            pltpu.SemaphoreType.DMA((4,)),
            pltpu.SemaphoreType.DMA((4,)),
            pltpu.SemaphoreType.DMA((4,)),
            pltpu.SemaphoreType.DMA((4,)),
            pltpu.SemaphoreType.DMA((4, 2)),
            pltpu.SemaphoreType.DMA((5,)),
            pltpu.SemaphoreType.DMA((2,)),
            pltpu.SemaphoreType.DMA((2,)),
        ],
        compiler_params=pltpu.CompilerParams(
            collective_id=0,
            has_side_effects=True,
            vmem_limit_bytes=125 * 512 * 1024,
        ),
    )(
        pos,
        start,
        q.reshape(flat),
        do.reshape(flat),
        o.reshape(flat),
        k,
        v,
        lse.T,
        pos.reshape(TOK // TILE, TILE),
    )
    return dq.reshape(q.shape) * 2, dk * 2, dv * 2


def solution(mesh):
    n_blk = mesh.shape["blk"]
    in_specs = (
        P("blk", "head", None),
        P("blk", "head", None),
        P("blk", "head", None),
        P("blk", None),
        P("blk", None),
        P("blk", "head"),
        P("blk"),
        P("blk"),
    )
    out_specs = (P("blk", "head", None), P("blk", None), P("blk", None))
    return jax.shard_map(
        functools.partial(call, n_blk),
        mesh=mesh,
        in_specs=in_specs,
        out_specs=out_specs,
        check_vma=False,
    )
```

time: 56 us -> 47.1 us (0.84)
  local copies, waits for them, and re-layouts: 5.46 us -> 0 us
  Pallas kernels: 49.6 us -> 44.7 us
  other arithmetic: 0 us -> 1.76 us
    unnamed x8 -> x0, local copies, waits for them, and re-layouts: 5.46 us -> none
    pallas_call x1, Pallas kernels: 49.6 us -> 44.7 us  [call(): pl.pallas_call(functools.partial(kernel, n_blk), out_shape=(pltpu.VMEM(fl...]
    mul x0 -> x2, other arithmetic: none -> 1.76 us  [call(): return (dq.reshape(q.shape) * 2, dk * 2, dv * 2)]
where the time goes in v1:
time: 47.1 us; the launch traced here: 47 us
  Pallas kernels  44.7 us (95%)
  other arithmetic  1.76 us (4%)
  between operations  0.64 us (1%)
    pallas_call x1, Pallas kernels, call(): pl.pallas_call(functools.partial(kernel, n_blk), out_shape=(pltpu.VMEM(fl...  44.7 us
    mul x2, other arithmetic, call(): return (dq.reshape(q.shape) * 2, dk * 2, dv * 2)  1.76 us

profile of v1, /device:TPU:1, one launch (start us, length us, event | category | flops | bytes accessed | tf_op | source)
XLA Modules:
  0.0 47.0 jit_solution(8249317849197496080)
XLA Ops:
  0.6 44.7 %shard_map.103 = (bf16[4096,128]{1,0:T(8,128)(2,1)S(1)}, bf16[512,128]{1,0:T(8,128)(2,1)S(1)}, bf16[512,128]{1,0:T(8,128)(2,1)S(1)}) custom-call(s32[512]{0:T(512)} %pos_in.1, s32[512]{0:T(512)} %start_in.1, bf16[4096,128]{1,0:T(8,128)(2,1)} %bitcast.7, bf16[4096,128]{1,0:T(8,128)(2,1)} %bitcast.8, bf16[4096,128]{1,0:T(8,128)(2,1)} %bitcast.9, ...), custom_call_target="tpu_custom_call" | custom-call | tf_op jit(solution)/shard_map/pallas_call | solution.py:423
  45.3 1.0 %multiply_bitcast_fusion = bf16[512,8,128]{2,1,0:T(8,128)(2,1)} fusion(bf16[4096,128]{1,0:T(8,128)(2,1)S(1)} %get-tuple-element.6), kind=kLoop, calls=%fused_computation | loop fusion | flops 524288 | bytes 2097152 | tf_op jit(solution)/shard_map/mul | solution.py:485
  46.3 0.7 %broadcast_multiply_fusion = (bf16[512,128]{1,0:T(8,128)(2,1)}, bf16[512,128]{1,0:T(8,128)(2,1)}) fusion(bf16[512,128]{1,0:T(8,128)(2,1)S(1)} %get-tuple-element.8, bf16[512,128]{1,0:T(8,128)(2,1)S(1)} %get-tuple-element.7), kind=kLoop, calls=%fused_computation.1 | loop fusion | flops 131072 | bytes 524288 | tf_op jit(solution)/shard_map/mul | solution.py:485

commit v2 on v1

--- a/solution.py
+++ b/solution.py
@@ -260,6 +260,7 @@
 
     lax.fori_loop(0, ROWS // 512, prepare, 0)
     dq[...] = jnp.zeros_like(dq)
+    start_kv(0, reach, 1, -reach)
 
     def work(slot):
         keys = kv.at[slot, 0:TOK, :]
@@ -318,7 +319,6 @@
 
         @pl.when(turn == 0)
         def _():
-            start_kv(0, reach, 1, -reach)
             own[...] = acc[...]
 
         @pl.when(jnp.logical_and(turn == 0, even))

time: 47.1 us -> 46.7 us (level)
  Pallas kernels: 44.7 us -> 44.2 us
where the time goes in v2:
time: 46.7 us; the launch traced here: 46.6 us
  Pallas kernels  44.2 us (95%)
  other arithmetic  1.76 us (4%)
  between operations  0.64 us (1%)
    pallas_call x1, Pallas kernels, call(): pl.pallas_call(functools.partial(kernel, n_blk), out_shape=(pltpu.VMEM(fl...  44.2 us
    mul x2, other arithmetic, call(): return (dq.reshape(q.shape) * 2, dk * 2, dv * 2)  1.76 us

profile of v2, /device:TPU:1, one launch (start us, length us, event | category | flops | bytes accessed | tf_op | source)
XLA Modules:
  0.0 46.6 jit_solution(10924422541804737910)
XLA Ops:
  0.6 44.2 %shard_map.103 = (bf16[4096,128]{1,0:T(8,128)(2,1)S(1)}, bf16[512,128]{1,0:T(8,128)(2,1)S(1)}, bf16[512,128]{1,0:T(8,128)(2,1)S(1)}) custom-call(s32[512]{0:T(512)} %pos_in.1, s32[512]{0:T(512)} %start_in.1, bf16[4096,128]{1,0:T(8,128)(2,1)} %bitcast.7, bf16[4096,128]{1,0:T(8,128)(2,1)} %bitcast.8, bf16[4096,128]{1,0:T(8,128)(2,1)} %bitcast.9, ...), custom_call_target="tpu_custom_call" | custom-call | tf_op jit(solution)/shard_map/pallas_call | solution.py:423
  44.8 1.0 %multiply_bitcast_fusion = bf16[512,8,128]{2,1,0:T(8,128)(2,1)} fusion(bf16[4096,128]{1,0:T(8,128)(2,1)S(1)} %get-tuple-element.6), kind=kLoop, calls=%fused_computation | loop fusion | flops 524288 | bytes 2097152 | tf_op jit(solution)/shard_map/mul | solution.py:485
  45.9 0.7 %broadcast_multiply_fusion = (bf16[512,128]{1,0:T(8,128)(2,1)}, bf16[512,128]{1,0:T(8,128)(2,1)}) fusion(bf16[512,128]{1,0:T(8,128)(2,1)S(1)} %get-tuple-element.8, bf16[512,128]{1,0:T(8,128)(2,1)S(1)} %get-tuple-element.7), kind=kLoop, calls=%fused_computation.1 | loop fusion | flops 131072 | bytes 524288 | tf_op jit(solution)/shard_map/mul | solution.py:485

commit v3 on v2

--- a/solution.py
+++ b/solution.py
@@ -115,6 +115,8 @@
     part_recv,
     mate_recv,
     last_sem,
+    far_send,
+    far_recv,
 ):
     blk, head = lax.axis_index("blk"), lax.axis_index("head")
     odd = lax.rem(blk, 2) == 1
@@ -197,6 +199,21 @@
             device(shift),
             MESH,
         )
+
+    pieces = [slice(0, TOK // 2), slice(TOK // 2, TOK)]
+
+    def far_copy(src, shift, across, i):
+        return pltpu.make_async_remote_copy(
+            part.at[src, lax.rem(head + across, 2), :, pieces[i]],
+            inbox.at[FAR + across, :, pieces[i]],
+            far_send.at[src - 1, across, i],
+            far_recv.at[across, i],
+            device(shift, across),
+            MESH,
+        )
+
+    def each_far(src, shift):
+        return [far_copy(src, shift, across, i) for i in range(2) for across in range(2)]
 
     def wait_part(dst):
         part_copy(0, dst, 0).wait_recv()
@@ -341,7 +358,8 @@
         @pl.when(jnp.logical_and(turn == 2, odd))
         def _():
             part[1] = low(acc[...])
-            send_halves(1, FAR, 3)
+            for copy in each_far(1, 3):
+                copy.start()
 
         @pl.when(jnp.logical_and(turn == 2, even))
         def _():
@@ -353,7 +371,8 @@
         def _():
             wait_mate(MATE)
             part[2] = low(acc[...] + full(mate_box[MATE]))
-            send_halves(2, FAR, 2)
+            for copy in each_far(2, 2):
+                copy.start()
 
         @pl.when(jnp.logical_and(turn == 3, even))
         def _():
@@ -378,16 +397,26 @@
         wait_part(NEAR + 1)
         half[...] += full(inbox[NEAR]) + full(inbox[NEAR + 1])
 
-    wait_part(FAR)
-    wait_part(FAR + 1)
-    total = half[...] + (full(inbox[FAR]) + full(inbox[FAR + 1]))
     factor = jnp.where(head == 0, SCALE * HALF, HALF)
-    grad_low[head] = low(jnp.swapaxes(total * factor, 0, 1))
-    last = pltpu.make_async_remote_copy(
-        grad_low.at[head], grad_low.at[head], last_sem.at[0], last_sem.at[1], device(0, 1), MESH
-    )
-    last.start()
-    last.wait()
+    lasts = []
+    for i, keys in enumerate(pieces):
+        for across in range(2):
+            far_copy(1, 0, across, i).wait_recv()
+        total = half[:, keys] + (full(inbox[FAR, :, keys]) + full(inbox[FAR + 1, :, keys]))
+        grad_low[head, keys, :] = low(jnp.swapaxes(total * factor, 0, 1))
+        lasts.append(
+            pltpu.make_async_remote_copy(
+                grad_low.at[head, keys],
+                grad_low.at[head, keys],
+                last_sem.at[0, i],
+                last_sem.at[1, i],
+                device(0, 1),
+                MESH,
+            )
+        )
+        lasts[i].start()
+    for last in lasts:
+        last.wait()
     dk_out[...] = grad_low[0]
     dv_out[...] = grad_low[1]
 
@@ -403,10 +432,8 @@
         wait_kv_send(1, 2, 2, -1)
         wait_kv_send(2, 3, 3, -1)
         mate_copy(0, MATE, -1).wait_send()
-        sent(1, FAR, 3)
-        sent(1, FAR + 1, 3, 1)
-        sent(2, FAR, 2)
-        sent(2, FAR + 1, 2, 1)
+        for copy in each_far(1, 3) + each_far(2, 2):
+            copy.wait_send()
 
     @pl.when(even)
     def _():
@@ -464,7 +491,9 @@
             pltpu.SemaphoreType.DMA((4, 2)),
             pltpu.SemaphoreType.DMA((5,)),
             pltpu.SemaphoreType.DMA((2,)),
-            pltpu.SemaphoreType.DMA((2,)),
+            pltpu.SemaphoreType.DMA((2, 2)),
+            pltpu.SemaphoreType.DMA((2, 2, 2)),
+            pltpu.SemaphoreType.DMA((2, 2)),
         ],
         compiler_params=pltpu.CompilerParams(
             collective_id=0,

time: 46.7 us -> 46.1 us (0.987)
  Pallas kernels: 44.2 us -> 43.6 us
    pallas_call x1, Pallas kernels: 44.2 us -> 43.6 us  [call(): pl.pallas_call(functools.partial(kernel, n_blk), out_shape=(pltpu.VMEM(fl...]
where the time goes in v3:
time: 46.1 us; the launch traced here: 46 us
  Pallas kernels  43.6 us (95%)
  other arithmetic  1.76 us (4%)
  between operations  0.64 us (1%)
    pallas_call x1, Pallas kernels, call(): pl.pallas_call(functools.partial(kernel, n_blk), out_shape=(pltpu.VMEM(fl...  43.6 us
    mul x2, other arithmetic, call(): return (dq.reshape(q.shape) * 2, dk * 2, dv * 2)  1.76 us

profile of v3, /device:TPU:1, one launch (start us, length us, event | category | flops | bytes accessed | tf_op | source)
XLA Modules:
  0.0 46.0 jit_solution(531988451718033554)
XLA Ops:
  0.6 43.6 %shard_map.103 = (bf16[4096,128]{1,0:T(8,128)(2,1)S(1)}, bf16[512,128]{1,0:T(8,128)(2,1)S(1)}, bf16[512,128]{1,0:T(8,128)(2,1)S(1)}) custom-call(s32[512]{0:T(512)} %pos_in.1, s32[512]{0:T(512)} %start_in.1, bf16[4096,128]{1,0:T(8,128)(2,1)} %bitcast.7, bf16[4096,128]{1,0:T(8,128)(2,1)} %bitcast.8, bf16[4096,128]{1,0:T(8,128)(2,1)} %bitcast.9, ...), custom_call_target="tpu_custom_call" | custom-call | tf_op jit(solution)/shard_map/pallas_call | solution.py:450
  44.3 1.0 %multiply_bitcast_fusion = bf16[512,8,128]{2,1,0:T(8,128)(2,1)} fusion(bf16[4096,128]{1,0:T(8,128)(2,1)S(1)} %get-tuple-element.6), kind=kLoop, calls=%fused_computation | loop fusion | flops 524288 | bytes 2097152 | tf_op jit(solution)/shard_map/mul | solution.py:514
  45.3 0.7 %broadcast_multiply_fusion = (bf16[512,128]{1,0:T(8,128)(2,1)}, bf16[512,128]{1,0:T(8,128)(2,1)}) fusion(bf16[512,128]{1,0:T(8,128)(2,1)S(1)} %get-tuple-element.8, bf16[512,128]{1,0:T(8,128)(2,1)S(1)} %get-tuple-element.7), kind=kLoop, calls=%fused_computation.1 | loop fusion | flops 131072 | bytes 524288 | tf_op jit(solution)/shard_map/mul | solution.py:514
